TPU v7x, 32 devices: a whole 2x2x4 slice. The times are simulated.
32 devices in a mesh: member: 8 (over z, y), band: 4 (over x, core).
Axes of the slice: x: 2, y: 2, z: 4, core: 2. Of those that a mesh axis runs over, the one named last changes fastest.
Arguments:
- spectral: float32 [128, 768, 768], P('member', 'band'), parts along dimension 0, may hold values from -6 to 6
- coupling: float32 [8192, 1024], P(('member', 'band')), parts along dimension 0, may hold values from 0.02 to 162, as said below
- quadratic: float32 [8192, 1024], P(('member', 'band')), parts along dimension 0, may hold values from -1.5 to 1.5
Outputs:
- tendency_spectral: float32 [128, 768, 768], P('member', 'band'), parts along dimension 0
There are 8 independent parts, one for each index of `member`. A program takes and returns all parts, laid end to end along the dimension named above; each array names one. Nothing has to cross between parts.
Inputs may be any that keep to these rules, and one draw needn't show every extreme that they name: `coupling`: positive.
All inputs are finite; a program needn't handle non-finite values.
Results may differ from a plain program's by a relative error of at most 0.00008.
Values sent between devices are 32-bit elements; how exact they have to be, the bound alone decides.
A program may use at most 128 MiB of HBM per device.

v0:
```python
import math
import jax
import jax.numpy as jnp
from jax import lax
from jax.sharding import PartitionSpec as P


def tables(cells, coeffs):
    half_count = coeffs // 2
    position = jnp.arange(cells, dtype=jnp.int32)
    column = jnp.arange(coeffs, dtype=jnp.int32)
    wavenumber = jnp.where(column < half_count, column, column - half_count)
    turns = position[:, None] * wavenumber[None, :] % cells
    angles = turns.astype(jnp.float32) * (2.0 * math.pi / cells)
    basis_table = jnp.where(column[None, :] < half_count, jnp.cos(angles), jnp.sin(angles))
    synthesis = basis_table / math.sqrt(half_count)
    factor = jnp.where(wavenumber == 0, 1.0, 2.0) * (math.sqrt(half_count) / cells)
    analysis = (basis_table * factor[None, :]).T
    return (synthesis, analysis)


def on_device(spectral, coupling, quadratic):
    high = lax.Precision.HIGHEST
    coeffs = spectral.shape[2]
    cells = coupling.shape[1]
    synthesis, analysis = tables(cells, coeffs)
    points = float(cells * cells)
    section = jnp.einsum("lab,yb->lay", spectral, synthesis, precision=high)
    turned = lax.all_to_all(section, "band", split_axis=2, concat_axis=1, tiled=True)
    grid = jnp.einsum("xa,lay->lyx", synthesis, turned, precision=high)
    product = coupling[None] * grid
    product, local_sum = (product, jnp.sum(product * product, axis=(1, 2)))
    total = lax.psum(local_sum, "band")
    scaled = product / jnp.sqrt(total / points + 1e-06)[:, None, None]
    tendency = scaled + quadratic[None] * scaled * scaled
    back = jnp.einsum("ax,lyx->lya", analysis, tendency, precision=high)
    returned = lax.all_to_all(back, "band", split_axis=2, concat_axis=1, tiled=True)
    return jnp.einsum("by,lya->lab", analysis, returned, precision=high)


def solution(mesh):
    placed = (P("member", "band", None), P(("member", "band"), None), P(("member", "band"), None))
    return jax.shard_map(
        on_device, mesh=mesh, in_specs=placed, out_specs=P("member", "band", None), check_vma=False
    )
```

profile of v0, /device:TPU:0, one launch (start us, length us, event | category | flops | bytes accessed | tf_op | source)
XLA Modules:
  0.0 669.1 jit_solution(13568946825027268618)
XLA Ops:
  0.0 12.7 %fusion.59 = f32[1024,768,1]{1,0,2:T(8,128)S(1)} fusion(s32[768]{0:T(1024)S(1)} %add_select_fusion.1, pred[768]{0:T(1024)(128)(4,1)S(1)} %iota_compare_fusion), kind=kLoop, calls=%fused_computation.20.clone.1 | loop fusion | flops 12582912 | bytes 3149568 | tf_op jit(solution)/shard_map/lab,yb->lay/dot_general | solution.py:28
  12.7 34.2 %convolution_bitcast_fusion = f32[16,192,1024]{2,1,0:T(8,128)} fusion(f32[16,192,768]{2,1,0:T(8,128)} %param.3, f32[1024,768,1]{1,0,2:T(8,128)S(1)} %fusion.59), kind=kOutput, calls=%fused_computation.11 | convolution fusion | flops 28991029248 | bytes 25165824 | tf_op jit(solution)/shard_map/lab,yb->lay/dot_general | solution.py:28
  46.9 17.7 %copy.15 = f32[16,192,1024]{1,0,2:T(8,128)} copy(f32[16,192,1024]{2,1,0:T(8,128)} %convolution_bitcast_fusion) | data formatting | bytes 25165824 | tf_op jit(solution)/shard_map/lab,yb->lay/dot_general | solution.py:28
  64.6 18.3 %all-to-all-start = ((f32[16,192,1024]{1,0,2:T(8,128)}), f32[16,192,1024]{1,0,2:T(8,128)}, u32[]{:S(2)}, u32[]{:S(2)}) async-start(f32[16,192,1024]{1,0,2:T(8,128)} %copy.15), calls=%async_computation | async-start | bytes 33554432 | tf_op jit(solution)/shard_map/all_to_all | solution.py:29
  83.0 12.4 %fusion.13.clone.4 = f32[1024,768,1]{1,0,2:T(8,128)S(1)} fusion(s32[768]{0:T(1024)S(1)} %add_select_fusion.1, pred[768]{0:T(1024)(128)(4,1)S(1)} %iota_compare_fusion), kind=kLoop, calls=%fused_computation.19.clone.clone.clone.1 | loop fusion | flops 12582912 | bytes 3149568 | tf_op jit(solution)/shard_map/reduce_sum | solution.py:32
  95.4 159.9 %all-to-all-done = f32[16,192,1024]{1,0,2:T(8,128)} async-done(((f32[16,192,1024]{1,0,2:T(8,128)}), f32[16,192,1024]{1,0,2:T(8,128)}, u32[]{:S(2)}, u32[]{:S(2)}) %all-to-all-start) | async-done | bytes 12582944 | tf_op jit(solution)/shard_map/all_to_all | solution.py:29
  255.3 14.5 %copy.23 = f32[16,192,4,256]{3,2,1,0:T(4,128)} copy(f32[16,192,4,256]{1,0,3,2:T(8,128)} %bitcast.2) | data formatting | bytes 25165824 | tf_op jit(solution)/shard_map/all_to_all | solution.py:29
  269.8 0.0 copy-start
  269.8 11.3 %copy.17 = f32[16,4,192,256]{3,2,1,0:T(8,128)} copy(f32[16,4,192,256]{3,1,2,0:T(4,128)} %bitcast.45) | data formatting | bytes 25165824 | tf_op jit(solution)/shard_map/all_to_all | solution.py:29
  281.1 0.0 copy-done
  281.1 83.8 %multiply_reduce_fusion = (f32[16]{0:T(128)S(1)}, f32[16,256,1024]{2,1,0:T(8,128)}) fusion(f32[256,1024]{1,0:T(8,128)S(1)} %copy-done, f32[16,768,256]{2,1,0:T(8,128)} %bitcast.46, f32[1024,768,1]{1,0,2:T(8,128)S(1)} %fusion.13.clone.4), kind=kOutput, calls=%fused_computation.3 | convolution fusion | flops 38667288576 | bytes 33554496 | tf_op jit(solution)/shard_map/xa,lay->lyx/dot_general | solution.py:30
  365.0 5.8 psum.7
  370.7 12.9 %multiply_add_fusion.5 = f32[16,256,1024]{2,1,0:T(8,128)} fusion(f32[16,256,1024]{2,1,0:T(8,128)} %get-tuple-element.6, f32[256,1024]{1,0:T(8,128)} %param.5, f32[16]{0:T(128)S(1)} %add_sqrt_fusion, f32[256,1024]{1,0:T(8,128)} %param.4), kind=kLoop, calls=%fused_computation.clone.clone.2 | loop fusion | flops 20971520 | bytes 35651648 | tf_op jit(solution)/shard_map/ax,lyx->lya/dot_general | solution.py:36
  383.7 58.5 %fusion = f32[16,256,768]{2,1,0:T(8,128)} fusion(f32[768]{0:T(1024)S(1)} %select_multiply_fusion, s32[768]{0:T(1024)S(1)} %add_select_fusion.1, pred[768]{0:T(1024)(128)(4,1)S(1)} %iota_compare_fusion, f32[16,256,1024]{2,1,0:T(8,128)} %multiply_add_fusion.5), kind=kOutput, calls=%fused_computation.1 | convolution fusion | flops 38667288576 | bytes 29367040 | tf_op jit(solution)/shard_map/ax,lyx->lya/dot_general | solution.py:36
  442.2 12.8 %copy.19 = f32[16,256,768]{1,0,2:T(8,128)} copy(f32[16,256,768]{2,1,0:T(8,128)} %fusion) | data formatting | bytes 25165824 | tf_op jit(solution)/shard_map/ax,lyx->lya/dot_general | solution.py:36
  455.0 6.5 all-to-all-start.1
  461.5 12.7 %fusion.61 = f32[1024,768,1]{1,0,2:T(8,128)S(1)} fusion(f32[768]{0:T(1024)S(1)} %select_multiply_fusion, s32[768]{0:T(1024)S(1)} %add_select_fusion.1, pred[768]{0:T(1024)(128)(4,1)S(1)} %iota_compare_fusion), kind=kLoop, calls=%fused_computation.16.clone.1 | loop fusion | flops 12582912 | bytes 3152640 | tf_op jit(solution)/shard_map/by,lya->lab/dot_general | solution.py:38
  474.2 125.2 %all-to-all-done.1 = f32[16,256,768]{1,0,2:T(8,128)} async-done(((f32[16,256,768]{1,0,2:T(8,128)}), f32[16,256,768]{1,0,2:T(8,128)}, u32[]{:S(2)}, u32[]{:S(2)}) %all-to-all-start.1) | async-done | bytes 12582944 | tf_op jit(solution)/shard_map/all_to_all | solution.py:37
  599.4 16.5 %copy.21 = f32[16,4,256,192]{2,1,3,0:T(4,128)} copy(f32[16,4,256,192]{2,0,3,1:T(8,128)} %bitcast.8) | data formatting | bytes 25165824 | tf_op jit(solution)/shard_map/all_to_all | solution.py:37
  615.9 15.7 %all_to_all.33 = f32[16,1024,192]{1,2,0:T(8,128)} reshape(f32[16,4,256,192]{2,1,3,0:T(4,128)} %copy.21) | data formatting | bytes 25165824 | tf_op jit(solution)/shard_map/all_to_all | solution.py:37
  631.6 37.1 %fusion.9 = f32[16,192,768]{2,1,0:T(8,128)} fusion(f32[16,1024,192]{1,2,0:T(8,128)} %all_to_all.33, f32[1024,768,1]{1,0,2:T(8,128)S(1)} %fusion.61), kind=kOutput, calls=%fused_computation.15 | convolution fusion | flops 28991029248 | bytes 25165824 | tf_op jit(solution)/shard_map/by,lya->lab/dot_general | solution.py:38
  (4 shorter events, 0.0 us)
Async XLA Ops:
  64.6 190.7 %all-to-all-start = ((f32[16,192,1024]{1,0,2:T(8,128)}), f32[16,192,1024]{1,0,2:T(8,128)}, u32[]{:S(2)}, u32[]{:S(2)}) async-start(f32[16,192,1024]{1,0,2:T(8,128)} %copy.15), calls=%async_computation | async-start | bytes 33554432 | tf_op jit(solution)/shard_map/all_to_all | solution.py:29
  269.8 11.3 %copy-start = (f32[256,1024]{1,0:T(8,128)S(1)}, f32[256,1024]{1,0:T(8,128)}, u32[]{:S(2)}) copy-start(f32[256,1024]{1,0:T(8,128)} %param.4) | copy-start | bytes 3145732
  455.0 144.4 %all-to-all-start.1 = ((f32[16,256,768]{1,0,2:T(8,128)}), f32[16,256,768]{1,0,2:T(8,128)}, u32[]{:S(2)}, u32[]{:S(2)}) async-start(f32[16,256,768]{1,0,2:T(8,128)} %copy.19), calls=%async_computation.1 | async-start | bytes 25165824 | tf_op jit(solution)/shard_map/all_to_all | solution.py:37
where the time goes:
time: 679 us; the launch traced here: 669 us
  waiting for transfers between devices  285 us (42%)
  matrix products  214 us (32%)
  local copies, waits for them, and re-layouts  88.5 us (13%)
  other arithmetic  50.8 us (7%)
  starting transfers between devices  24.9 us (4%)
    all_to_all x1, waiting for transfers between devices, on_device(): lax.all_to_all(section, 'band', split_axis=2, concat_axis=1, tiled=True)  160 us
    all_to_all x1, waiting for transfers between devices, on_device(): lax.all_to_all(back, 'band', split_axis=2, concat_axis=1, tiled=True)  125 us
    dot_general x1, matrix products, on_device(): grid = jnp.einsum('xa,lay->lyx', synthesis, turned, precision=high)  83.8 us
    dot_general x1, matrix products, on_device(): back = jnp.einsum('ax,lyx->lya', analysis, tendency, precision=high)  58.5 us
    dot_general x1, matrix products, on_device(): return jnp.einsum('by,lya->lab', analysis, returned, precision=high)  37.1 us
    dot_general x1, matrix products, on_device(): section = jnp.einsum('lab,yb->lay', spectral, synthesis, precision=high)  34.2 us
    all_to_all x2, local copies, waits for them, and re-layouts, on_device(): lax.all_to_all(back, 'band', split_axis=2, concat_axis=1, tiled=True)  32.2 us
    all_to_all x2, local copies, waits for them, and re-layouts, on_device(): lax.all_to_all(section, 'band', split_axis=2, concat_axis=1, tiled=True)  25.8 us
  transfers between devices with their start and end apart: 2, of which 2 were waited for; matrix products, arithmetic and copies ran while one was open for 4% of the time, Pallas kernels for 0%

commit v1 on v0

--- a/solution.py
+++ b/solution.py
@@ -26,7 +26,10 @@
     synthesis, analysis = tables(cells, coeffs)
     points = float(cells * cells)
     section = jnp.einsum("lab,yb->lay", spectral, synthesis, precision=high)
-    turned = lax.all_to_all(section, "band", split_axis=2, concat_axis=1, tiled=True)
+    turned = jnp.concatenate(
+        lax.all_to_all(jnp.stack(jnp.split(section, lax.axis_size("band"), axis=2)), "band", 0, 0),
+        axis=1,
+    )
     grid = jnp.einsum("xa,lay->lyx", synthesis, turned, precision=high)
     product = coupling[None] * grid
     product, local_sum = (product, jnp.sum(product * product, axis=(1, 2)))

time: 679 us -> 617 us (0.909)
  waiting for transfers between devices: 285 us -> 241 us
  local copies, waits for them, and re-layouts: 88.5 us -> 64.7 us
  other arithmetic: 50.8 us -> 58.5 us
    all_to_all x1, waiting for transfers between devices: 160 us -> 116 us  [on_device(): lax.all_to_all(jnp.stack(jnp.split(section, lax.axis_size('band'), axis=2...]
    all_to_all x2 -> x0, local copies, waits for them, and re-layouts: 25.8 us -> none  [on_device(): lax.all_to_all(section, 'band', split_axis=2, concat_axis=1, tiled=True)]
    dot_general x1 -> x0, local copies, waits for them, and re-layouts: 17.7 us -> none  [on_device(): section = jnp.einsum('lab,yb->lay', spectral, synthesis, precision=high)]
    reshape x0 -> x1, local copies, waits for them, and re-layouts: none -> 10.7 us  [on_device(): jnp.concatenate(lax.all_to_all(jnp.stack(jnp.split(section, lax.axis_size...]
    another operation x0 -> x1, local copies, waits for them, and re-layouts: none -> 9 us  [on_device(): jnp.stack(jnp.split(section, lax.axis_size('band'), axis=2))]
    another operation x0 -> x1, other arithmetic: none -> 7.79 us  [on_device(): jnp.stack(jnp.split(section, lax.axis_size('band'), axis=2))]
where the time goes in v1:
time: 617 us; the launch traced here: 607 us
  waiting for transfers between devices  241 us (39%)
  matrix products  214 us (35%)
  local copies, waits for them, and re-layouts  64.7 us (10%)
  other arithmetic  58.5 us (9%)
  starting transfers between devices  22.9 us (4%)
    all_to_all x1, waiting for transfers between devices, on_device(): lax.all_to_all(back, 'band', split_axis=2, concat_axis=1, tiled=True)  125 us
    all_to_all x1, waiting for transfers between devices, on_device(): lax.all_to_all(jnp.stack(jnp.split(section, lax.axis_size('band'), axis=2...  116 us
    dot_general x1, matrix products, on_device(): grid = jnp.einsum('xa,lay->lyx', synthesis, turned, precision=high)  83.8 us
    dot_general x1, matrix products, on_device(): back = jnp.einsum('ax,lyx->lya', analysis, tendency, precision=high)  58.6 us
    dot_general x1, matrix products, on_device(): return jnp.einsum('by,lya->lab', analysis, returned, precision=high)  37.1 us
    dot_general x1, matrix products, on_device(): section = jnp.einsum('lab,yb->lay', spectral, synthesis, precision=high)  34.2 us
    all_to_all x2, local copies, waits for them, and re-layouts, on_device(): lax.all_to_all(back, 'band', split_axis=2, concat_axis=1, tiled=True)  32.2 us
    all_to_all x1, starting transfers between devices, on_device(): lax.all_to_all(jnp.stack(jnp.split(section, lax.axis_size('band'), axis=2...  16.3 us
  transfers between devices with their start and end apart: 2, of which 2 were waited for; matrix products, arithmetic and copies ran while one was open for 4% of the time, Pallas kernels for 0%

profile of v1, /device:TPU:0, one launch (start us, length us, event | category | flops | bytes accessed | tf_op | source)
XLA Modules:
  0.0 607.5 jit_solution(4162077328491786197)
XLA Ops:
  0.0 12.7 %fusion.59 = f32[1024,768,1]{1,0,2:T(8,128)S(1)} fusion(s32[768]{0:T(1024)S(1)} %add_select_fusion.1, pred[768]{0:T(1024)(128)(4,1)S(1)} %iota_compare_fusion), kind=kLoop, calls=%fused_computation.25.clone.1 | loop fusion | flops 12582912 | bytes 3149568 | tf_op jit(solution)/shard_map/lab,yb->lay/dot_general | solution.py:28
  12.7 34.2 %convolution_bitcast_fusion = f32[16,192,1024]{2,1,0:T(8,128)} fusion(f32[16,192,768]{2,1,0:T(8,128)} %param.3, f32[1024,768,1]{1,0,2:T(8,128)S(1)} %fusion.59), kind=kOutput, calls=%fused_computation.12 | convolution fusion | flops 28991029248 | bytes 25165824 | tf_op jit(solution)/shard_map/lab,yb->lay/dot_general | solution.py:28
  46.9 9.0 %slice_bitcast_fusion.3 = (f32[1,16,192,256]{3,2,1,0:T(8,128)S(1)}, f32[1,16,192,256]{3,2,1,0:T(8,128)S(1)}, f32[1,16,192,256]{3,2,1,0:T(8,128)}, f32[1,16,192,256]{3,2,1,0:T(8,128)}) fusion(f32[16,192,1024]{2,1,0:T(8,128)} %convolution_bitcast_fusion), kind=kLoop, calls=%fused_computation.19 | loop fusion | bytes 25165824 | tf_op jit(solution)/shard_map/stack | solution.py:30
  55.9 7.8 %pad_maximum_fusion = f32[4,16,192,256]{3,2,1,0:T(8,128)} fusion(f32[1,16,192,256]{3,2,1,0:T(8,128)S(1)} %get-tuple-element.6, f32[1,16,192,256]{3,2,1,0:T(8,128)} %get-tuple-element.7, f32[1,16,192,256]{3,2,1,0:T(8,128)} %get-tuple-element.8, f32[1,16,192,256]{3,2,1,0:T(8,128)S(1)} %get-tuple-element.5), kind=kLoop, calls=%fused_computation.5 | loop fusion | flops 9437184 | bytes 25165824 | tf_op jit(solution)/shard_map/stack | solution.py:30
  63.7 16.3 %all-to-all-start = ((f32[4,16,192,256]{3,2,1,0:T(8,128)}), f32[4,16,192,256]{3,2,1,0:T(8,128)}, u32[]{:S(2)}, u32[]{:S(2)}) async-start(f32[4,16,192,256]{3,2,1,0:T(8,128)} %pad_maximum_fusion), calls=%async_computation | async-start | bytes 25165824 | tf_op jit(solution)/shard_map/all_to_all | solution.py:30
  80.1 12.4 %fusion.13.clone.4 = f32[1024,768,1]{1,0,2:T(8,128)S(1)} fusion(s32[768]{0:T(1024)S(1)} %add_select_fusion.1, pred[768]{0:T(1024)(128)(4,1)S(1)} %iota_compare_fusion), kind=kLoop, calls=%fused_computation.24.clone.clone.clone.1 | loop fusion | flops 12582912 | bytes 3149568 | tf_op jit(solution)/shard_map/reduce_sum | solution.py:35
  92.5 116.3 %all-to-all-done = f32[4,16,192,256]{3,2,1,0:T(8,128)} async-done(((f32[4,16,192,256]{3,2,1,0:T(8,128)}), f32[4,16,192,256]{3,2,1,0:T(8,128)}, u32[]{:S(2)}, u32[]{:S(2)}) %all-to-all-start) | async-done | bytes 12582944 | tf_op jit(solution)/shard_map/all_to_all | solution.py:30
  208.8 0.0 copy-start
  208.8 10.7 %copy.9 = f32[16,4,192,256]{3,2,1,0:T(8,128)} copy(f32[16,4,192,256]{3,2,0,1:T(8,128)} %bitcast.6) | data formatting | bytes 25165824 | tf_op jit(solution)/shard_map/reshape | solution.py:29
  219.5 0.0 copy-done
  219.5 83.8 %multiply_reduce_fusion = (f32[16]{0:T(128)S(1)}, f32[16,256,1024]{2,1,0:T(8,128)}) fusion(f32[256,1024]{1,0:T(8,128)S(1)} %copy-done, f32[16,768,256]{2,1,0:T(8,128)} %bitcast.52, f32[1024,768,1]{1,0,2:T(8,128)S(1)} %fusion.13.clone.4), kind=kOutput, calls=%fused_computation.3 | convolution fusion | flops 38667288576 | bytes 33554496 | tf_op jit(solution)/shard_map/xa,lay->lyx/dot_general | solution.py:33
  303.3 5.8 psum.7
  309.1 12.9 %multiply_add_fusion.5 = f32[16,256,1024]{2,1,0:T(8,128)} fusion(f32[16,256,1024]{2,1,0:T(8,128)} %get-tuple-element.10, f32[256,1024]{1,0:T(8,128)} %param.5, f32[16]{0:T(128)S(1)} %add_sqrt_fusion, f32[256,1024]{1,0:T(8,128)} %param.4), kind=kLoop, calls=%fused_computation.clone.clone.2 | loop fusion | flops 20971520 | bytes 35651648 | tf_op jit(solution)/shard_map/ax,lyx->lya/dot_general | solution.py:39
  322.0 58.6 %fusion = f32[16,256,768]{2,1,0:T(8,128)} fusion(f32[768]{0:T(1024)S(1)} %select_multiply_fusion, s32[768]{0:T(1024)S(1)} %add_select_fusion.1, pred[768]{0:T(1024)(128)(4,1)S(1)} %iota_compare_fusion, f32[16,256,1024]{2,1,0:T(8,128)} %multiply_add_fusion.5), kind=kOutput, calls=%fused_computation.1 | convolution fusion | flops 38667288576 | bytes 29367040 | tf_op jit(solution)/shard_map/ax,lyx->lya/dot_general | solution.py:39
  380.6 12.8 %copy.11 = f32[16,256,768]{1,0,2:T(8,128)} copy(f32[16,256,768]{2,1,0:T(8,128)} %fusion) | data formatting | bytes 25165824 | tf_op jit(solution)/shard_map/ax,lyx->lya/dot_general | solution.py:39
  393.4 6.5 %all-to-all-start.1 = ((f32[16,256,768]{1,0,2:T(8,128)}), f32[16,256,768]{1,0,2:T(8,128)}, u32[]{:S(2)}, u32[]{:S(2)}) async-start(f32[16,256,768]{1,0,2:T(8,128)} %copy.11), calls=%async_computation.1 | async-start | bytes 25165824 | tf_op jit(solution)/shard_map/all_to_all | solution.py:40
  399.9 12.7 %fusion.61 = f32[1024,768,1]{1,0,2:T(8,128)S(1)} fusion(f32[768]{0:T(1024)S(1)} %select_multiply_fusion, s32[768]{0:T(1024)S(1)} %add_select_fusion.1, pred[768]{0:T(1024)(128)(4,1)S(1)} %iota_compare_fusion), kind=kLoop, calls=%fused_computation.21.clone.1 | loop fusion | flops 12582912 | bytes 3152640 | tf_op jit(solution)/shard_map/by,lya->lab/dot_general | solution.py:41
  412.6 125.2 %all-to-all-done.1 = f32[16,256,768]{1,0,2:T(8,128)} async-done(((f32[16,256,768]{1,0,2:T(8,128)}), f32[16,256,768]{1,0,2:T(8,128)}, u32[]{:S(2)}, u32[]{:S(2)}) %all-to-all-start.1) | async-done | bytes 12582944 | tf_op jit(solution)/shard_map/all_to_all | solution.py:40
  537.8 16.5 %copy.13 = f32[16,4,256,192]{2,1,3,0:T(4,128)} copy(f32[16,4,256,192]{2,0,3,1:T(8,128)} %bitcast.11) | data formatting | bytes 25165824 | tf_op jit(solution)/shard_map/all_to_all | solution.py:40
  554.3 15.7 %all_to_all.20 = f32[16,1024,192]{1,2,0:T(8,128)} reshape(f32[16,4,256,192]{2,1,3,0:T(4,128)} %copy.13) | data formatting | bytes 25165824 | tf_op jit(solution)/shard_map/all_to_all | solution.py:40
  569.9 37.1 %fusion.9 = f32[16,192,768]{2,1,0:T(8,128)} fusion(f32[16,1024,192]{1,2,0:T(8,128)} %all_to_all.20, f32[1024,768,1]{1,0,2:T(8,128)S(1)} %fusion.61), kind=kOutput, calls=%fused_computation.20 | convolution fusion | flops 28991029248 | bytes 25165824 | tf_op jit(solution)/shard_map/by,lya->lab/dot_general | solution.py:41
  (4 shorter events, 0.0 us)
Async XLA Ops:
  63.7 145.1 %all-to-all-start = ((f32[4,16,192,256]{3,2,1,0:T(8,128)}), f32[4,16,192,256]{3,2,1,0:T(8,128)}, u32[]{:S(2)}, u32[]{:S(2)}) async-start(f32[4,16,192,256]{3,2,1,0:T(8,128)} %pad_maximum_fusion), calls=%async_computation | async-start | bytes 25165824 | tf_op jit(solution)/shard_map/all_to_all | solution.py:30
  208.8 10.7 %copy-start = (f32[256,1024]{1,0:T(8,128)S(1)}, f32[256,1024]{1,0:T(8,128)}, u32[]{:S(2)}) copy-start(f32[256,1024]{1,0:T(8,128)} %param.4) | copy-start | bytes 3145732
  393.4 144.4 %all-to-all-start.1 = ((f32[16,256,768]{1,0,2:T(8,128)}), f32[16,256,768]{1,0,2:T(8,128)}, u32[]{:S(2)}, u32[]{:S(2)}) async-start(f32[16,256,768]{1,0,2:T(8,128)} %copy.11), calls=%async_computation.1 | async-start | bytes 25165824 | tf_op jit(solution)/shard_map/all_to_all | solution.py:40
